TPU v7x, 32 devices: a whole 2x2x4 slice. The times are simulated.
32 devices in a mesh: section: 4 (over y, core), seq: 8 (over z, x).
Axes of the slice: x: 2, y: 2, z: 4, core: 2. Of those that a mesh axis runs over, the one named last changes fastest.
Arguments:
- stream: bfloat16 [4, 512, 1024], P('section', 'seq'), may hold values from -1.5 to 1.5
- queries: bfloat16 [4, 512, 1024], P('section', 'seq'), may hold values from -8 to 8
- key_rows: bfloat16 [4, 512, 1024], P('section', 'seq'), may hold values from -8 to 8
- values: bfloat16 [4, 512, 1024], P('section', 'seq'), may hold values from -36 to 36
- incoming: bfloat16 [512, 1024], P('seq'), may hold values from -1.5 to 1.5
Outputs:
- updated: bfloat16 [4, 512, 1024], P('section', 'seq')
- received: bfloat16 [4, 512, 1024], P('section', 'seq')
All inputs are finite; a program needn't handle non-finite values.
Results may differ from a plain program's by a relative error of at most 0.0054.
Values may be sent and summed in bfloat16 or wider, within the bound.
A program may use at most 64 MiB of HBM per device.

v0:
```python
import functools

import jax
import jax.numpy as jnp
from jax import lax
from jax.experimental import pallas as pl
from jax.experimental.pallas import tpu as pltpu
from jax.sharding import PartitionSpec as P

HEAD_SIZE = 128
GROUP = 8
LOG2_E = 1.4426950408889634
MESH = pl.DeviceIdType.MESH


def flipped(place, mask):
    result, weight = 0, 1
    while weight < GROUP:
        bit = lax.rem(lax.div(place, weight), 2)
        result = result + weight * ((1 - bit) if mask & weight else bit)
        weight *= 2
    return result


def kernel(
    sections,
    stream_hbm, query_hbm, key_hbm, value_hbm, incoming_hbm,
    both_ref,
    stream_own, query_own, key_own, value_own,
    query_all, key_all, value_all, result, attended,
    load_sem, own_sem, send_sem, recv_sem, back_send, back_recv, pass_send, pass_recv, first_sem, known_sem,
):
    updated_ref, received_ref = both_ref.at[0], both_ref.at[1]
    section = lax.axis_index("section")
    seq = lax.axis_index("seq")
    me = lax.rem(seq, GROUP)
    base = seq - me
    width = query_all.shape[2]
    masks = [1, 6, 7, 4, 5, 3, 2]
    place = {mask: flipped(me, mask) for mask in range(GROUP)}

    def columns_of(partner):
        return pl.ds(pl.multiple_of((partner - base) * width, HEAD_SIZE), width)

    def columns(mask):
        return pl.ds(pl.multiple_of(place[mask] * width, HEAD_SIZE), width)

    sources = (key_hbm, value_hbm, query_hbm)
    held = (key_own, value_own, query_own)
    whole = (key_all, value_all, query_all)
    loads = [pltpu.make_async_copy(sources[i], held[i], load_sem.at[i]) for i in range(3)]
    loads.append(pltpu.make_async_copy(stream_hbm, stream_own, load_sem.at[3]))
    owns = [
        pltpu.make_async_copy(sources[i].at[:, columns(0)], whole[i].at[0], own_sem.at[i])
        for i in range(3)
    ]
    loads[0].start()
    loads[1].start()
    loads[2].start()

    barrier = pltpu.get_barrier_semaphore()
    for mask in (4, 2, 1):
        pl.semaphore_signal(
            barrier, inc=1, device_id={"seq": base + place[mask]}, device_id_type=MESH
        )
    previous = lax.rem(section + sections - 1, sections)
    pl.semaphore_signal(barrier, inc=1, device_id={"section": previous}, device_id_type=MESH)
    for own in owns:
        own.start()
    loads[3].start()
    first = pltpu.make_async_copy(incoming_hbm, received_ref, first_sem)

    @pl.when(section == 0)
    def _():
        first.start()

    def exchange(kind, mask, partner=None):
        partner = base + place[mask] if partner is None else partner
        return pltpu.make_async_remote_copy(
            src_ref=held[kind].at[:, columns_of(partner)],
            dst_ref=whole[kind].at[mask],
            send_sem=send_sem.at[kind, mask],
            recv_sem=recv_sem.at[kind, mask],
            device_id={"seq": partner},
            device_id_type=MESH,
        )

    def giving_back(mask, partner=None):
        partner = base + place[mask] if partner is None else partner
        return pltpu.make_async_remote_copy(
            src_ref=result.at[mask],
            dst_ref=attended.at[mask],
            send_sem=back_send.at[mask],
            recv_sem=back_recv.at[mask],
            device_id={"seq": partner},
            device_id_type=MESH,
        )

    def passing(mask):
        return pltpu.make_async_remote_copy(
            src_ref=updated_ref.at[:, columns(mask)],
            dst_ref=received_ref.at[:, columns(mask)],
            send_sem=pass_send.at[mask],
            recv_sem=pass_recv.at[mask],
            device_id={"section": lax.rem(section + 1, sections)},
            device_id_type=MESH,
        )

    def tell(index, mask):
        pl.semaphore_signal(
            known_sem.at[index], inc=1,
            device_id={"seq": base + place[mask]}, device_id_type=MESH,
        )

    def send(kinds, *to):
        for mask in to:
            for kind in kinds:
                exchange(kind, mask).start()

    pl.semaphore_wait(barrier, 4)
    tell(0, 1)
    tell(1, 2)
    for kind in range(3):
        loads[kind].wait()
    send((0, 1), 4, 1)
    pl.semaphore_wait(known_sem.at[0], 1)
    send((0, 1), 5)
    pl.semaphore_wait(known_sem.at[1], 1)
    tell(2, 1)
    send((0, 1), 6)
    pl.semaphore_wait(known_sem.at[2], 1)
    send((0, 1), 7, 3, 2)
    send((2,), *masks)
    for own in owns:
        own.wait()
    loads[3].wait()
    for kind in range(2):
        for mask in masks:
            exchange(kind, mask).wait_recv()

    factor = HEAD_SIZE ** -0.5 * LOG2_E

    def attend(mask):
        for start in range(0, width, HEAD_SIZE):
            feats = pl.ds(start, HEAD_SIZE)
            keys = key_all[:, :, feats].reshape(-1, HEAD_SIZE)
            vals = value_all[:, :, feats].reshape(-1, HEAD_SIZE)
            scores = lax.dot_general(
                query_all[mask, :, feats], keys, (((1,), (1,)), ((), ())),
                preferred_element_type=jnp.float32,
            )
            highest = jnp.max(scores, axis=-1, keepdims=True)
            exponent = jnp.exp2((scores - highest) * factor)
            totals = jnp.sum(exponent, axis=-1, keepdims=True)
            summed = jnp.dot(
                exponent.astype(jnp.bfloat16), vals, preferred_element_type=jnp.float32
            )
            result[mask, :, feats] = (summed * (1.0 / totals)).astype(jnp.bfloat16)

    def update(mask, piece):
        cols = columns(mask)
        updated_ref[:, cols] = (
            stream_own[:, cols].astype(jnp.float32) + piece.astype(jnp.float32)
        ).astype(jnp.bfloat16)

        @pl.when(section < sections - 1)
        def _():
            passing(mask).start()

    def serve(mask, partner):
        exchange(2, mask, partner).wait_recv()
        attend(mask)
        giving_back(mask, partner).start()

    @pl.when(me > 0)
    def _():
        serve(me, base)

    for mask in masks:

        @pl.when(me != mask)
        def _():
            serve(mask, base + place[mask])

    attend(0)
    update(0, result[0])
    for mask in masks:
        giving_back(mask).wait_recv()
        update(mask, attended[mask])

    for mask in masks:
        for kind in range(3):
            exchange(kind, mask).wait_send()
        giving_back(mask).wait_send()

    @pl.when(section < sections - 1)
    def _():
        for mask in range(GROUP):
            passing(mask).wait_send()

    @pl.when(section > 0)
    def _():
        for mask in range(GROUP):
            passing(mask).wait_recv()

    @pl.when(section == 0)
    def _():
        first.wait()


def per_device(sections, stream, queries, key_rows, values, incoming):
    rows, features = incoming.shape
    width = features // GROUP
    block = pltpu.VMEM((2, rows, features), jnp.bfloat16)
    own = pltpu.VMEM((rows, features), jnp.bfloat16)
    whole = pltpu.VMEM((GROUP, rows, width), jnp.bfloat16)
    both = pl.pallas_call(
        functools.partial(kernel, sections),
        out_shape=block,
        in_specs=[pl.BlockSpec(memory_space=pl.ANY)] * 5,
        out_specs=pl.BlockSpec(memory_space=pltpu.VMEM),
        scratch_shapes=[own] * 4 + [whole] * 5 + [
            pltpu.SemaphoreType.DMA((4,)),
            pltpu.SemaphoreType.DMA((3,)),
            pltpu.SemaphoreType.DMA((3, GROUP)),
            pltpu.SemaphoreType.DMA((3, GROUP)),
            pltpu.SemaphoreType.DMA((GROUP,)),
            pltpu.SemaphoreType.DMA((GROUP,)),
            pltpu.SemaphoreType.DMA((GROUP,)),
            pltpu.SemaphoreType.DMA((GROUP,)),
            pltpu.SemaphoreType.DMA,
            pltpu.SemaphoreType.REGULAR((3,)),
        ],
        compiler_params=pltpu.CompilerParams(collective_id=0, has_side_effects=True),
    )(stream[0], queries[0], key_rows[0], values[0], incoming)
    return both[:1], both[1:]


def solution(mesh):
    placed = (
        P("section", "seq", None),
        P("section", "seq", None),
        P("section", "seq", None),
        P("section", "seq", None),
        P("seq", None),
    )
    return jax.shard_map(
        functools.partial(per_device, mesh.shape["section"]),
        mesh=mesh,
        in_specs=placed,
        out_specs=(P("section", "seq", None), P("section", "seq", None)),
        check_vma=False,
    )
```

profile of v0, /device:TPU:3, one launch (start us, length us, event | category | flops | bytes accessed | tf_op | source)
XLA Modules:
  0.0 22.0 jit_solution(17558793878018599944)
XLA Ops:
  0.6 20.7 %shard_map.68 = bf16[2,64,1024]{2,1,0:T(8,128)(2,1)S(1)} custom-call(bf16[64,1024]{1,0:T(8,128)(2,1)} %bitcast.4, bf16[64,1024]{1,0:T(8,128)(2,1)} %bitcast.5, bf16[64,1024]{1,0:T(8,128)(2,1)} %bitcast.6, bf16[64,1024]{1,0:T(8,128)(2,1)} %bitcast.7, bf16[64,1024]{1,0:T(8,128)(2,1)} %incoming_hbm.1), custom_call_target="tpu_custom_call" | custom-call | tf_op jit(solution)/shard_map/pallas_call | solution.py:217
  21.3 0.7 %fusion = (bf16[1,64,1024]{2,1,0:T(8,128)(2,1)}, bf16[1,64,1024]{2,1,0:T(8,128)(2,1)}) fusion(bf16[2,64,1024]{2,1,0:T(8,128)(2,1)S(1)} %shard_map.68), kind=kLoop, calls=%fused_computation | loop fusion | bytes 524288 | tf_op jit(solution)/shard_map/slice | solution.py:236
where the time goes:
time: 22.2 us; the launch traced here: 22 us
  Pallas kernels  20.7 us (93%)
  local copies, waits for them, and re-layouts  0.72 us (3%)
  between operations  0.64 us (3%)
    pallas_call x1, Pallas kernels, per_device(): pl.pallas_call(functools.partial(kernel, sections), out_shape=block, in_s...  20.7 us
    slice x1, local copies, waits for them, and re-layouts, per_device(): return (both[:1], both[1:])  0.72 us

commit v1 on v0

v1 whole, which is shorter than its diff:
```python
import functools

import jax
import jax.numpy as jnp
from jax import lax
from jax.experimental import pallas as pl
from jax.experimental.pallas import tpu as pltpu
from jax.sharding import PartitionSpec as P

HEAD_SIZE = 128
GROUP = 8
LOG2_E = 1.4426950408889634
MESH = pl.DeviceIdType.MESH
KEY_VALUE = (0, 1)
QUERY = (2,)
ALL = (0, 1, 2)
QUERY_FIRST = (2, 0, 1)
SEND_ORDER = (
    ((4, KEY_VALUE), (1, KEY_VALUE), (5, KEY_VALUE), (6, KEY_VALUE), (7, KEY_VALUE), (3, KEY_VALUE), (2, KEY_VALUE), (1, QUERY), (6, QUERY), (7, QUERY), (4, QUERY), (5, QUERY), (3, QUERY), (2, QUERY)),
    ((4, KEY_VALUE), (1, KEY_VALUE), (5, KEY_VALUE), (6, KEY_VALUE), (7, KEY_VALUE), (3, KEY_VALUE), (2, KEY_VALUE), (1, QUERY), (6, QUERY), (7, QUERY), (4, QUERY), (5, QUERY), (3, QUERY), (2, QUERY)),
    ((4, KEY_VALUE), (1, KEY_VALUE), (5, KEY_VALUE), (6, KEY_VALUE), (7, KEY_VALUE), (3, KEY_VALUE), (2, KEY_VALUE), (1, QUERY), (6, QUERY), (7, QUERY), (4, QUERY), (5, QUERY), (3, QUERY), (2, QUERY)),
    ((4, KEY_VALUE), (1, KEY_VALUE), (5, KEY_VALUE), (6, KEY_VALUE), (7, KEY_VALUE), (3, KEY_VALUE), (2, KEY_VALUE), (1, QUERY), (6, QUERY), (7, QUERY), (4, QUERY), (5, QUERY), (3, QUERY), (2, QUERY)),
    ((4, KEY_VALUE), (1, KEY_VALUE), (5, KEY_VALUE), (6, KEY_VALUE), (7, KEY_VALUE), (3, KEY_VALUE), (2, KEY_VALUE), (1, QUERY), (6, QUERY), (7, QUERY), (4, QUERY), (5, QUERY), (3, QUERY), (2, QUERY)),
    ((4, KEY_VALUE), (1, KEY_VALUE), (5, KEY_VALUE), (6, KEY_VALUE), (7, KEY_VALUE), (3, KEY_VALUE), (2, KEY_VALUE), (1, QUERY), (6, QUERY), (7, QUERY), (4, QUERY), (5, QUERY), (3, QUERY), (2, QUERY)),
    ((4, KEY_VALUE), (1, KEY_VALUE), (5, KEY_VALUE), (6, KEY_VALUE), (7, KEY_VALUE), (3, KEY_VALUE), (2, KEY_VALUE), (1, QUERY), (6, QUERY), (7, QUERY), (4, QUERY), (5, QUERY), (3, QUERY), (2, QUERY)),
    ((4, KEY_VALUE), (1, KEY_VALUE), (5, KEY_VALUE), (6, KEY_VALUE), (7, KEY_VALUE), (3, KEY_VALUE), (2, KEY_VALUE), (1, QUERY), (6, QUERY), (7, QUERY), (4, QUERY), (5, QUERY), (3, QUERY), (2, QUERY)),
    ((4, KEY_VALUE), (1, KEY_VALUE), (5, KEY_VALUE), (6, KEY_VALUE), (7, KEY_VALUE), (3, KEY_VALUE), (2, KEY_VALUE), (1, QUERY), (6, QUERY), (7, QUERY), (4, QUERY), (5, QUERY), (3, QUERY), (2, QUERY)),
    ((4, KEY_VALUE), (1, KEY_VALUE), (5, KEY_VALUE), (6, KEY_VALUE), (7, KEY_VALUE), (3, KEY_VALUE), (2, KEY_VALUE), (1, QUERY), (6, QUERY), (7, QUERY), (4, QUERY), (5, QUERY), (3, QUERY), (2, QUERY)),
    ((4, KEY_VALUE), (1, KEY_VALUE), (5, KEY_VALUE), (6, KEY_VALUE), (7, KEY_VALUE), (3, KEY_VALUE), (2, KEY_VALUE), (1, QUERY), (6, QUERY), (7, QUERY), (4, QUERY), (5, QUERY), (3, QUERY), (2, QUERY)),
    ((4, KEY_VALUE), (1, KEY_VALUE), (5, KEY_VALUE), (6, KEY_VALUE), (7, KEY_VALUE), (3, KEY_VALUE), (2, KEY_VALUE), (1, QUERY), (6, QUERY), (7, QUERY), (4, QUERY), (5, QUERY), (3, QUERY), (2, QUERY)),
    ((4, KEY_VALUE), (1, KEY_VALUE), (5, KEY_VALUE), (6, KEY_VALUE), (7, KEY_VALUE), (3, KEY_VALUE), (2, KEY_VALUE), (1, QUERY), (6, QUERY), (7, QUERY), (4, QUERY), (5, QUERY), (3, QUERY), (2, QUERY)),
    ((4, KEY_VALUE), (1, KEY_VALUE), (5, KEY_VALUE), (6, KEY_VALUE), (7, KEY_VALUE), (3, KEY_VALUE), (2, KEY_VALUE), (1, QUERY), (6, QUERY), (7, QUERY), (4, QUERY), (5, QUERY), (3, QUERY), (2, QUERY)),
    ((4, KEY_VALUE), (1, KEY_VALUE), (5, KEY_VALUE), (6, KEY_VALUE), (7, KEY_VALUE), (3, KEY_VALUE), (2, KEY_VALUE), (1, QUERY), (6, QUERY), (7, QUERY), (4, QUERY), (5, QUERY), (3, QUERY), (2, QUERY)),
    ((4, KEY_VALUE), (1, KEY_VALUE), (5, KEY_VALUE), (6, KEY_VALUE), (7, KEY_VALUE), (3, KEY_VALUE), (2, KEY_VALUE), (1, QUERY), (6, QUERY), (7, QUERY), (4, QUERY), (5, QUERY), (3, QUERY), (2, QUERY)),
)
SERVE_ORDER = (((3, 1), (2, 1), (1, 1), (0, 1)), ((2, 1), (0, 1), (1, 1), (3, 1)), ((2, 1), (0, 1), (1, 1), (3, 1)), ((3, 1), (2, 1), (1, 1), (0, 1)))
UPDATE_ORDER = ((0, 1, 2, 3),) * 4


def flipped(place, mask):
    result, weight = 0, 1
    while weight < GROUP:
        bit = lax.rem(lax.div(place, weight), 2)
        result = result + weight * ((1 - bit) if mask & weight else bit)
        weight *= 2
    return result


def kernel(
    sections,
    stream_hbm, query_hbm, key_hbm, value_hbm, incoming_hbm,
    both_ref,
    stream_own, held, key_all, value_all, query_all, result, attended,
    load_sem, send_sem, recv_sem, query_sem, back_sem, known_sem,
):
    updated_ref, received_ref = both_ref.at[0], both_ref.at[1]
    section = lax.axis_index("section")
    seq = lax.axis_index("seq")
    me = lax.rem(seq, GROUP)
    base = seq - me
    row = lax.div(me, 2)
    width = query_all.shape[2]
    place = {mask: flipped(me, mask) for mask in range(GROUP)}
    others = pl.ds(1, GROUP - 1)

    def columns(mask):
        return pl.ds(pl.multiple_of(place[mask] * width, HEAD_SIZE), width)

    whole = (key_all, value_all, query_all)
    loads = [
        pltpu.make_async_copy(source, held.at[kind], load_sem.at[0])
        for kind, source in enumerate((key_hbm, value_hbm, query_hbm))
    ]
    for load in loads:
        load.start()

    side = lax.rem(me, 2)
    barrier = pltpu.get_barrier_semaphore()
    for mask in range(1, GROUP):
        later_row = place[mask] > me + 1 - side
        if mask == 1:
            greets = (side == 0) | (row == 0)
        elif mask % 2:
            greets = later_row & (side == 0)
        else:
            greets = later_row

        @pl.when(greets)
        def _():
            pl.semaphore_signal(
                barrier, inc=1, device_id={"seq": base + place[mask]}, device_id_type=MESH
            )

    @pl.when(section < sections - 1)
    def _():
        pl.semaphore_signal(barrier, inc=1, device_id={"section": section + 1}, device_id_type=MESH)

    stream_load = pltpu.make_async_copy(stream_hbm, stream_own, load_sem.at[1])
    stream_load.start()
    first = pltpu.make_async_copy(incoming_hbm, received_ref, load_sem.at[2])

    @pl.when(section == 0)
    def _():
        first.start()

    def exchange(kind, mask):
        return pltpu.make_async_remote_copy(
            src_ref=held.at[kind, :, columns(mask)],
            dst_ref=whole[kind].at[mask],
            send_sem=send_sem.at[kind],
            recv_sem=query_sem.at[mask // 2] if kind == 2 else recv_sem.at[kind],
            device_id={"seq": base + place[mask]},
            device_id_type=MESH,
        )

    def giving_back(mask):
        return pltpu.make_async_remote_copy(
            src_ref=result.at[mask],
            dst_ref=attended.at[mask],
            send_sem=send_sem.at[3],
            recv_sem=back_sem.at[mask // 2],
            device_id={"seq": base + place[mask]},
            device_id_type=MESH,
        )

    def passing(cols):
        return pltpu.make_async_remote_copy(
            src_ref=updated_ref.at[:, cols],
            dst_ref=received_ref.at[:, cols],
            send_sem=send_sem.at[4],
            recv_sem=recv_sem.at[2],
            device_id={"section": lax.rem(section + 1, sections)},
            device_id_type=MESH,
        )

    def landed(ref, sem):
        pltpu.make_async_copy(ref, ref, sem).wait()

    greeted = jnp.where(side == 0, jnp.maximum(row, 1), 2 * row + 1)
    pl.semaphore_wait(barrier, greeted + jnp.where(section > 0, 1, 0))
    for mask in (6, 4, 2, 7, 5, 3, 1):
        earlier_row = place[mask] < me - side
        if mask == 1:
            answers = (side == 1) & (row > 0)
        elif mask % 2:
            answers = earlier_row & (side == 1)
        else:
            answers = earlier_row

        @pl.when(answers)
        def _():
            pl.semaphore_signal(
                known_sem.at[mask], inc=1,
                device_id={"seq": base + place[mask]}, device_id_type=MESH,
            )

    @pl.when(section > 0)
    def _():
        pl.semaphore_signal(
            known_sem.at[0], inc=1, device_id={"section": section - 1}, device_id_type=MESH
        )

    def by_place(orders, run):
        for number, order in enumerate(orders):
            if order:

                @pl.when(me + GROUP * lax.rem(section, 2) == number)
                def _():
                    run(number % GROUP, order)

    def notices(mine, mask):
        theirs = mine ^ mask
        if theirs // 2 > mine // 2:
            return mask - mask % 2 * (mine % 2)
        if mine % 2 == 0 and theirs % 2 and mine > 0:
            return 1
        return 0

    def send(mine, order):
        met = {0}
        for mask, kinds in order:
            notice = notices(mine, mask)
            if notice not in met:
                met.add(notice)
                pl.semaphore_wait(known_sem.at[notice], 1)
            for kind in kinds:
                exchange(kind, mask).start()

    def by_row(orders, run):
        for order in sorted(set(orders)):
            rows = [number for number, its in enumerate(orders) if its == order]
            here = row == rows[0]
            for number in rows[1:]:
                here = here | (row == number)

            @pl.when(here)
            def _():
                run(order)

    landed(held, load_sem.at[0])
    by_place(SEND_ORDER, send)
    for kind in range(3):
        whole[kind][0] = held[kind, :, columns(0)]
    landed(stream_own, load_sem.at[1])
    landed(key_all.at[others], recv_sem.at[0])
    landed(value_all.at[others], recv_sem.at[1])

    factor = HEAD_SIZE ** -0.5 * LOG2_E

    def attend(pair, count):
        at = pl.ds(2 * pair, 2 * count)
        for start in range(0, width, HEAD_SIZE):
            feats = pl.ds(start, HEAD_SIZE)
            keys = key_all[:, :, feats].reshape(-1, HEAD_SIZE)
            vals = value_all[:, :, feats].reshape(-1, HEAD_SIZE)
            scores = lax.dot_general(
                query_all[at, :, feats].reshape(-1, HEAD_SIZE), keys, (((1,), (1,)), ((), ())),
                preferred_element_type=jnp.float32,
            )
            highest = jnp.max(scores, axis=-1, keepdims=True)
            exponent = jnp.exp2((scores - highest) * factor)
            totals = jnp.sum(exponent, axis=-1, keepdims=True)
            summed = jnp.dot(
                exponent.astype(jnp.bfloat16), vals, preferred_element_type=jnp.float32
            )
            out = (summed * (1.0 / totals)).astype(jnp.bfloat16)
            result[at, :, feats] = out.reshape(2 * count, -1, HEAD_SIZE)

    def pieces(pair):
        return pl.ds(2 * pair, 2) if pair else pl.ds(1, 1)

    def serve(order):
        for pair, count in order:
            for number in range(pair, pair + count):
                landed(query_all.at[pieces(number)], query_sem.at[number])
            attend(pair, count)
            for mask in range(2 * pair, 2 * (pair + count)):
                if mask:
                    giving_back(mask).start()

    by_row(SERVE_ORDER, serve)

    def update(mask, piece):
        cols = columns(mask)
        updated_ref[:, cols] = (
            stream_own[:, cols].astype(jnp.float32) + piece.astype(jnp.float32)
        ).astype(jnp.bfloat16)

    def finish(order):
        for pair in order:
            landed(attended.at[pieces(pair)], back_sem.at[pair])
            update(2 * pair, attended[2 * pair] if pair else result[0])
            update(2 * pair + 1, attended[2 * pair + 1])

            @pl.when(section < sections - 1)
            def _():
                low = jnp.minimum(place[2 * pair], place[2 * pair + 1])
                passing(pl.ds(pl.multiple_of(low * width, HEAD_SIZE), 2 * width)).start()

    @pl.when(section < sections - 1)
    def _():
        pl.semaphore_wait(known_sem.at[0], 1)

    by_row(UPDATE_ORDER, finish)

    for kind in range(4):
        landed(key_all.at[others], send_sem.at[kind])

    @pl.when(section < sections - 1)
    def _():
        landed(updated_ref, send_sem.at[4])

    @pl.when(section > 0)
    def _():
        landed(received_ref, recv_sem.at[2])

    @pl.when(section == 0)
    def _():
        first.wait()


def per_device(sections, stream, queries, key_rows, values, incoming):
    rows, features = incoming.shape
    width = features // GROUP
    whole = pltpu.VMEM((GROUP, rows, width), jnp.bfloat16)
    both = pl.pallas_call(
        functools.partial(kernel, sections),
        out_shape=pltpu.VMEM((2, rows, features), jnp.bfloat16),
        in_specs=[pl.BlockSpec(memory_space=pl.ANY)] * 5,
        out_specs=pl.BlockSpec(memory_space=pltpu.VMEM),
        scratch_shapes=[
            pltpu.VMEM((rows, features), jnp.bfloat16),
            pltpu.VMEM((3, rows, features), jnp.bfloat16),
        ] + [whole] * 5 + [
            pltpu.SemaphoreType.DMA((3,)),
            pltpu.SemaphoreType.DMA((5,)),
            pltpu.SemaphoreType.DMA((3,)),
            pltpu.SemaphoreType.DMA((GROUP // 2,)),
            pltpu.SemaphoreType.DMA((GROUP // 2,)),
            pltpu.SemaphoreType.REGULAR((GROUP,)),
        ],
        compiler_params=pltpu.CompilerParams(collective_id=0, has_side_effects=True),
    )(stream[0], queries[0], key_rows[0], values[0], incoming)
    return both[:1], both[1:]


def solution(mesh):
    placed = (
        P("section", "seq", None),
        P("section", "seq", None),
        P("section", "seq", None),
        P("section", "seq", None),
        P("seq", None),
    )
    return jax.shard_map(
        functools.partial(per_device, mesh.shape["section"]),
        mesh=mesh,
        in_specs=placed,
        out_specs=(P("section", "seq", None), P("section", "seq", None)),
        check_vma=False,
    )
```

time: 22.2 us -> 22.3 us (level)
  the two profiles are of different devices: /device:TPU:3 before, /device:TPU:0 now
where the time goes in v1:
time: 22.3 us; the launch traced here: 21.9 us
  Pallas kernels  20.5 us (92%)
  local copies, waits for them, and re-layouts  0.72 us (3%)
  between operations  0.64 us (3%)
    pallas_call x1, Pallas kernels, per_device(): pl.pallas_call(functools.partial(kernel, sections), out_shape=pltpu.VMEM(...  20.5 us
    slice x1, local copies, waits for them, and re-layouts, per_device(): return (both[:1], both[1:])  0.72 us

profile of v1, /device:TPU:0, one launch (start us, length us, event | category | flops | bytes accessed | tf_op | source)
XLA Modules:
  0.0 21.9 jit_solution(18230274154722166474)
XLA Ops:
  0.6 20.5 %shard_map.68 = bf16[2,64,1024]{2,1,0:T(8,128)(2,1)S(1)} custom-call(bf16[64,1024]{1,0:T(8,128)(2,1)} %bitcast.4, bf16[64,1024]{1,0:T(8,128)(2,1)} %bitcast.5, bf16[64,1024]{1,0:T(8,128)(2,1)} %bitcast.6, bf16[64,1024]{1,0:T(8,128)(2,1)} %bitcast.7, bf16[64,1024]{1,0:T(8,128)(2,1)} %incoming_hbm.1), custom_call_target="tpu_custom_call" | custom-call | tf_op jit(solution)/shard_map/pallas_call | solution.py:286
  21.1 0.7 %fusion = (bf16[1,64,1024]{2,1,0:T(8,128)(2,1)}, bf16[1,64,1024]{2,1,0:T(8,128)(2,1)}) fusion(bf16[2,64,1024]{2,1,0:T(8,128)(2,1)S(1)} %shard_map.68), kind=kLoop, calls=%fused_computation | loop fusion | bytes 524288 | tf_op jit(solution)/shard_map/slice | solution.py:304

commit v2 on v1

v2 whole, which is shorter than its diff:
```python
import functools

import jax
import jax.numpy as jnp
from jax import lax
from jax.experimental import pallas as pl
from jax.experimental.pallas import tpu as pltpu
from jax.sharding import PartitionSpec as P

HEAD_SIZE = 128
GROUP = 8
WORKERS = (2, 3, 4, 5)
LOG2_E = 1.4426950408889634
MESH = pl.DeviceIdType.MESH
KEY_VALUE, QUERY, ALL = (0, 1), (2,), (0, 1, 2)
SEND_ORDER = (
    ((2, QUERY), (3, KEY_VALUE), (3, QUERY), (4, QUERY), (5, QUERY), (4, KEY_VALUE), (5, KEY_VALUE), (2, KEY_VALUE)),
    ((3, QUERY), (2, KEY_VALUE), (2, QUERY), (5, QUERY), (4, QUERY), (5, KEY_VALUE), (4, KEY_VALUE), (3, KEY_VALUE)),
    ((4, KEY_VALUE), (5, KEY_VALUE), (3, KEY_VALUE), (4, QUERY), (5, QUERY), (3, QUERY)),
    ((5, KEY_VALUE), (4, KEY_VALUE), (2, KEY_VALUE), (5, QUERY), (4, QUERY), (2, QUERY)),
    ((2, KEY_VALUE), (3, KEY_VALUE), (5, KEY_VALUE), (2, QUERY), (3, QUERY), (5, QUERY)),
    ((3, KEY_VALUE), (2, KEY_VALUE), (4, KEY_VALUE), (3, QUERY), (2, QUERY), (4, QUERY)),
    ((2, KEY_VALUE), (3, KEY_VALUE), (4, KEY_VALUE), (5, KEY_VALUE), (2, QUERY), (3, QUERY), (4, QUERY), (5, QUERY)),
    ((3, KEY_VALUE), (2, KEY_VALUE), (5, KEY_VALUE), (4, KEY_VALUE), (3, QUERY), (2, QUERY), (5, QUERY), (4, QUERY)),
    ((None, 500), (2, KEY_VALUE), (3, KEY_VALUE), (4, KEY_VALUE), (5, KEY_VALUE), (None, 1000), (4, QUERY), (5, QUERY), (2, QUERY), (3, QUERY)),
    ((None, 500), (3, KEY_VALUE), (2, KEY_VALUE), (5, KEY_VALUE), (4, KEY_VALUE), (None, 1000), (5, QUERY), (4, QUERY), (3, QUERY), (2, QUERY)),
    ((None, 500), (4, KEY_VALUE), (5, KEY_VALUE), (3, KEY_VALUE), (None, 1000), (4, QUERY), (5, QUERY), (3, QUERY)),
    ((None, 500), (5, KEY_VALUE), (4, KEY_VALUE), (2, KEY_VALUE), (None, 1000), (5, QUERY), (4, QUERY), (2, QUERY)),
    ((None, 500), (2, KEY_VALUE), (3, KEY_VALUE), (5, KEY_VALUE), (None, 1000), (2, QUERY), (3, QUERY), (5, QUERY)),
    ((None, 500), (3, KEY_VALUE), (2, KEY_VALUE), (4, KEY_VALUE), (None, 1000), (3, QUERY), (2, QUERY), (4, QUERY)),
    ((None, 500), (2, KEY_VALUE), (3, KEY_VALUE), (4, KEY_VALUE), (5, KEY_VALUE), (None, 1000), (2, QUERY), (3, QUERY), (4, QUERY), (5, QUERY)),
    ((None, 500), (3, KEY_VALUE), (2, KEY_VALUE), (5, KEY_VALUE), (4, KEY_VALUE), (None, 1000), (3, QUERY), (2, QUERY), (5, QUERY), (4, QUERY)),
)
LATE_ORDER = (
    (),
    (),
    (),
    (),
    (),
    (),
    (),
    (),
    (),
    (),
    (),
    (),
    (),
    (),
    (),
    (),
)
SERVE_ORDER = (((1, 1), (3, 1), (2, 1), (0, 1)), ((2, 1), (3, 1), (0, 1), (1, 1)))
FINISH_ORDER = ((2, 3, 4, 5), (2, 3, 4, 5), (2, 3, 4, 5), (2, 3, 4, 5))


def notice(mine, theirs):
    if theirs // 2 > mine // 2:
        return theirs if mine % 2 == 0 else theirs | 1
    if mine % 2 == 0 and theirs % 2 and mine > 0:
        return mine + 1
    return None


def notices(mine):
    return {notice(mine, theirs) for theirs in WORKERS if theirs != mine} - {None}


def kernel(
    sections,
    stream_hbm, query_hbm, key_hbm, value_hbm, incoming_hbm,
    both_ref,
    stream_own, held, gathered, result, attended,
    load_sem, send_sem, recv_sem, query_sem, back_sem, known_sem,
):
    updated_ref, received_ref = both_ref.at[0], both_ref.at[1]
    key_all, value_all, query_all = (gathered.at[kind] for kind in range(3))
    section = lax.axis_index("section")
    seq = lax.axis_index("seq")
    me = lax.rem(seq, GROUP)
    base = seq - me
    row, side = lax.div(me, 2), lax.rem(me, 2)
    width = gathered.shape[3]
    others = pl.ds(1, GROUP - 1)
    working = (me >= WORKERS[0]) & (me <= WORKERS[-1])

    loads = [
        pltpu.make_async_copy(source, held.at[kind], load_sem.at[0])
        for kind, source in enumerate((key_hbm, value_hbm, query_hbm))
    ]
    for load in loads:
        load.start()

    def here(run):
        for mine in range(GROUP):

            @pl.when(me == mine)
            def _():
                run(mine)

    def signal(sem, place):
        pl.semaphore_signal(sem, inc=1, device_id={"seq": base + place}, device_id_type=MESH)

    barrier = pltpu.get_barrier_semaphore()

    def greet(mine):
        for theirs in range(GROUP):
            later = theirs // 2 > mine // 2 and (mine % 2 == 0 or theirs % 2)
            if later or theirs == mine + 1 - mine % 2 * 2 and (mine % 2 == 0 or mine == 1):
                signal(barrier, theirs)

    here(greet)

    @pl.when(section < sections - 1)
    def _():
        pl.semaphore_signal(barrier, inc=1, device_id={"section": section + 1}, device_id_type=MESH)

    stream_load = pltpu.make_async_copy(stream_hbm, stream_own, load_sem.at[1])
    stream_load.start()

    @pl.when(section == 0)
    def _():
        pltpu.make_async_copy(incoming_hbm, received_ref, recv_sem.at[1]).start()

    def exchange(kind, mine, theirs):
        return pltpu.make_async_remote_copy(
            src_ref=held.at[kind, :, pl.ds((theirs - WORKERS[0]) * width, width)],
            dst_ref=gathered.at[kind, mine ^ theirs],
            send_sem=send_sem.at[3 if kind == 2 else 0],
            recv_sem=query_sem.at[(mine ^ theirs) // 2] if kind == 2 else recv_sem.at[0],
            device_id={"seq": base + theirs},
            device_id_type=MESH,
        )

    def giving_back(mask):
        place = 0
        for weight in (1, 2, 4):
            bit = lax.rem(lax.div(me, weight), 2)
            place = place + weight * ((1 - bit) if mask & weight else bit)
        return pltpu.make_async_remote_copy(
            src_ref=result.at[mask],
            dst_ref=attended.at[me - WORKERS[0]],
            send_sem=send_sem.at[1],
            recv_sem=back_sem.at[me - WORKERS[0]],
            device_id={"seq": base + place},
            device_id_type=MESH,
        )

    def passing(cols):
        return pltpu.make_async_remote_copy(
            src_ref=updated_ref.at[:, cols],
            dst_ref=received_ref.at[:, cols],
            send_sem=send_sem.at[2],
            recv_sem=recv_sem.at[1],
            device_id={"section": lax.rem(section + 1, sections)},
            device_id_type=MESH,
        )

    def landed(ref, sem):
        pltpu.make_async_copy(ref, ref, sem).wait()

    greeted = jnp.where(side == 0, jnp.maximum(row, 1), 2 * row + 1)
    pl.semaphore_wait(barrier, greeted + jnp.where(section > 0, 1, 0))

    def answer(mine):
        for theirs in range(GROUP):
            if mine in notices(theirs):
                signal(known_sem.at[mine ^ theirs], theirs)

    here(answer)

    @pl.when(section > 0)
    def _():
        pl.semaphore_signal(
            known_sem.at[0], inc=1, device_id={"section": section - 1}, device_id_type=MESH
        )

    landed(held, load_sem.at[0])
    def send(orders, earlier):
        for number, order in enumerate(orders):
            mine, met = number % GROUP, {None}
            for theirs, _ in earlier[number]:
                if theirs is not None:
                    met.add(notice(mine, theirs))
            if order:

                @pl.when(me + GROUP * lax.rem(section, 2) == number)
                def _():
                    for theirs, kinds in order:
                        if theirs is None:
                            pl.delay(kinds)
                            continue
                        shown = notice(mine, theirs)
                        if shown not in met:
                            met.add(shown)
                            pl.semaphore_wait(known_sem.at[mine ^ shown], 1)
                        for kind in kinds:
                            exchange(kind, mine, theirs).start()

    send(SEND_ORDER, [()] * len(SEND_ORDER))

    factor = HEAD_SIZE ** -0.5 * LOG2_E

    def attend(pair, count):
        at = pl.ds(2 * pair, 2 * count)
        for start in range(0, width, 2 * HEAD_SIZE):
            heads = [pl.ds(start + offset, HEAD_SIZE) for offset in (0, HEAD_SIZE)]
            scores = [
                lax.dot_general(
                    query_all[at, :, head].reshape(-1, HEAD_SIZE),
                    key_all[:, :, head].reshape(-1, HEAD_SIZE),
                    (((1,), (1,)), ((), ())),
                    preferred_element_type=jnp.float32,
                )
                for head in heads
            ]
            highest = [jnp.max(its, axis=-1, keepdims=True) for its in scores]
            exponent = [jnp.exp2((its - top) * factor) for its, top in zip(scores, highest)]
            totals = [jnp.sum(its, axis=-1, keepdims=True) for its in exponent]
            summed = [
                jnp.dot(
                    its.astype(jnp.bfloat16), value_all[:, :, head].reshape(-1, HEAD_SIZE),
                    preferred_element_type=jnp.float32,
                )
                for its, head in zip(exponent, heads)
            ]
            for its, total, head in zip(summed, totals, heads):
                out = (its * (1.0 / total)).astype(jnp.bfloat16)
                result[at, :, head] = out.reshape(2 * count, -1, HEAD_SIZE)

    @pl.when(working)
    def _():
        own = pl.ds(pl.multiple_of((me - WORKERS[0]) * width, HEAD_SIZE), width)
        for kind in range(3):
            gathered[kind, 0] = held[kind, :, own]
        landed(gathered.at[pl.ds(0, 2), others], recv_sem.at[0])

    @pl.when(jnp.logical_not(working))
    def _():
        landed(held.at[pl.ds(0, 2)], send_sem.at[0])

    send(LATE_ORDER, SEND_ORDER)

    for number, order in enumerate(SERVE_ORDER):

        @pl.when(row == WORKERS[0] // 2 + number)
        def _():
            for pair, count in order:
                for its in range(pair, pair + count):
                    landed(query_all.at[pl.ds(2 * its, 2) if its else pl.ds(1, 1)], query_sem.at[its])
                attend(pair, count)
                for mask in range(2 * pair, 2 * (pair + count)):
                    if mask:
                        giving_back(mask).start()

    landed(stream_own, load_sem.at[1])

    @pl.when(section < sections - 1)
    def _():
        pl.semaphore_wait(known_sem.at[0], 1)

    def finish(worker):
        cols = pl.ds((worker - WORKERS[0]) * width, width)

        def update(piece):
            updated_ref[:, cols] = (
                stream_own[:, cols].astype(jnp.float32) + piece.astype(jnp.float32)
            ).astype(jnp.bfloat16)

        @pl.when(me == worker)
        def _():
            update(result[0])

        @pl.when(me != worker)
        def _():
            landed(attended.at[worker - WORKERS[0]], back_sem.at[worker - WORKERS[0]])
            update(attended[worker - WORKERS[0]])

        @pl.when(section < sections - 1)
        def _():
            passing(cols).start()

    for order in sorted(set(FINISH_ORDER)):
        chosen = functools.reduce(
            jnp.logical_or, [row == number for number, its in enumerate(FINISH_ORDER) if its == order]
        )

        @pl.when(chosen)
        def _():
            for worker in order:
                finish(worker)

    @pl.when(working)
    def _():
        most = pl.ds(0, (len(WORKERS) - 1) * width)
        landed(held.at[pl.ds(0, 2), :, most], send_sem.at[0])
        landed(held.at[2, :, most], send_sem.at[3])
        landed(result.at[others], send_sem.at[1])

    @pl.when(jnp.logical_not(working))
    def _():
        landed(held.at[2], send_sem.at[3])

    @pl.when(section < sections - 1)
    def _():
        landed(updated_ref, send_sem.at[2])

    landed(received_ref, recv_sem.at[1])


def per_device(sections, stream, queries, key_rows, values, incoming):
    rows, features = incoming.shape
    width = features // len(WORKERS)
    both = pl.pallas_call(
        functools.partial(kernel, sections),
        out_shape=pltpu.VMEM((2, rows, features), jnp.bfloat16),
        in_specs=[pl.BlockSpec(memory_space=pl.ANY)] * 5,
        out_specs=pl.BlockSpec(memory_space=pltpu.VMEM),
        scratch_shapes=[
            pltpu.VMEM((rows, features), jnp.bfloat16),
            pltpu.VMEM((3, rows, features), jnp.bfloat16),
            pltpu.VMEM((3, GROUP, rows, width), jnp.bfloat16),
            pltpu.VMEM((GROUP, rows, width), jnp.bfloat16),
            pltpu.VMEM((len(WORKERS), rows, width), jnp.bfloat16),
            pltpu.SemaphoreType.DMA((2,)),
            pltpu.SemaphoreType.DMA((4,)),
            pltpu.SemaphoreType.DMA((2,)),
            pltpu.SemaphoreType.DMA((GROUP // 2,)),
            pltpu.SemaphoreType.DMA((len(WORKERS),)),
            pltpu.SemaphoreType.REGULAR((GROUP,)),
        ],
        compiler_params=pltpu.CompilerParams(collective_id=0, has_side_effects=True),
    )(stream[0], queries[0], key_rows[0], values[0], incoming)
    return both[:1], both[1:]


def solution(mesh):
    placed = (
        P("section", "seq", None),
        P("section", "seq", None),
        P("section", "seq", None),
        P("section", "seq", None),
        P("seq", None),
    )
    return jax.shard_map(
        functools.partial(per_device, mesh.shape["section"]),
        mesh=mesh,
        in_specs=placed,
        out_specs=(P("section", "seq", None), P("section", "seq", None)),
        check_vma=False,
    )
```

time: 22.3 us -> 21.6 us (0.969); the launches traced: 21.9 us -> 21.5 us
  Pallas kernels: 20.5 us -> 20.1 us
    pallas_call x1, Pallas kernels: 20.5 us -> 20.1 us  [per_device(): pl.pallas_call(functools.partial(kernel, sections), out_shape=pltpu.VMEM(...]
where the time goes in v2:
time: 21.6 us; the launch traced here: 21.5 us
  Pallas kernels  20.1 us (93%)
  local copies, waits for them, and re-layouts  0.72 us (3%)
  between operations  0.64 us (3%)
    pallas_call x1, Pallas kernels, per_device(): pl.pallas_call(functools.partial(kernel, sections), out_shape=pltpu.VMEM(...  20.1 us
    slice x1, local copies, waits for them, and re-layouts, per_device(): return (both[:1], both[1:])  0.72 us

profile of v2, /device:TPU:0, one launch (start us, length us, event | category | flops | bytes accessed | tf_op | source)
XLA Modules:
  0.0 21.5 jit_solution(2669673414874278062)
XLA Ops:
  0.6 20.1 %shard_map.68 = bf16[2,64,1024]{2,1,0:T(8,128)(2,1)S(1)} custom-call(bf16[64,1024]{1,0:T(8,128)(2,1)} %bitcast.4, bf16[64,1024]{1,0:T(8,128)(2,1)} %bitcast.5, bf16[64,1024]{1,0:T(8,128)(2,1)} %bitcast.6, bf16[64,1024]{1,0:T(8,128)(2,1)} %bitcast.7, bf16[64,1024]{1,0:T(8,128)(2,1)} %incoming_hbm.1), custom_call_target="tpu_custom_call" | custom-call | tf_op jit(solution)/shard_map/pallas_call | solution.py:313
  20.8 0.7 %fusion = (bf16[1,64,1024]{2,1,0:T(8,128)(2,1)}, bf16[1,64,1024]{2,1,0:T(8,128)(2,1)}) fusion(bf16[2,64,1024]{2,1,0:T(8,128)(2,1)S(1)} %shard_map.68), kind=kLoop, calls=%fused_computation | loop fusion | bytes 524288 | tf_op jit(solution)/shard_map/slice | solution.py:333

commit v3 on v2

--- a/solution.py
+++ b/solution.py
@@ -22,14 +22,14 @@
     ((3, KEY_VALUE), (2, KEY_VALUE), (4, KEY_VALUE), (3, QUERY), (2, QUERY), (4, QUERY)),
     ((2, KEY_VALUE), (3, KEY_VALUE), (4, KEY_VALUE), (5, KEY_VALUE), (2, QUERY), (3, QUERY), (4, QUERY), (5, QUERY)),
     ((3, KEY_VALUE), (2, KEY_VALUE), (5, KEY_VALUE), (4, KEY_VALUE), (3, QUERY), (2, QUERY), (5, QUERY), (4, QUERY)),
-    ((None, 500), (2, KEY_VALUE), (3, KEY_VALUE), (4, KEY_VALUE), (5, KEY_VALUE), (None, 1000), (4, QUERY), (5, QUERY), (2, QUERY), (3, QUERY)),
-    ((None, 500), (3, KEY_VALUE), (2, KEY_VALUE), (5, KEY_VALUE), (4, KEY_VALUE), (None, 1000), (5, QUERY), (4, QUERY), (3, QUERY), (2, QUERY)),
-    ((None, 500), (4, KEY_VALUE), (5, KEY_VALUE), (3, KEY_VALUE), (None, 1000), (4, QUERY), (5, QUERY), (3, QUERY)),
-    ((None, 500), (5, KEY_VALUE), (4, KEY_VALUE), (2, KEY_VALUE), (None, 1000), (5, QUERY), (4, QUERY), (2, QUERY)),
-    ((None, 500), (2, KEY_VALUE), (3, KEY_VALUE), (5, KEY_VALUE), (None, 1000), (2, QUERY), (3, QUERY), (5, QUERY)),
-    ((None, 500), (3, KEY_VALUE), (2, KEY_VALUE), (4, KEY_VALUE), (None, 1000), (3, QUERY), (2, QUERY), (4, QUERY)),
-    ((None, 500), (2, KEY_VALUE), (3, KEY_VALUE), (4, KEY_VALUE), (5, KEY_VALUE), (None, 1000), (2, QUERY), (3, QUERY), (4, QUERY), (5, QUERY)),
-    ((None, 500), (3, KEY_VALUE), (2, KEY_VALUE), (5, KEY_VALUE), (4, KEY_VALUE), (None, 1000), (3, QUERY), (2, QUERY), (5, QUERY), (4, QUERY)),
+    ((None, 500), (2, KEY_VALUE), (3, KEY_VALUE), (4, KEY_VALUE), (5, KEY_VALUE), (4, QUERY), (5, QUERY), (2, QUERY), (3, QUERY)),
+    ((None, 500), (3, KEY_VALUE), (2, KEY_VALUE), (5, KEY_VALUE), (4, KEY_VALUE), (5, QUERY), (4, QUERY), (3, QUERY), (2, QUERY)),
+    ((None, 500), (4, KEY_VALUE), (5, KEY_VALUE), (3, KEY_VALUE), (4, QUERY), (5, QUERY), (3, QUERY)),
+    ((None, 500), (5, KEY_VALUE), (4, KEY_VALUE), (2, KEY_VALUE), (5, QUERY), (4, QUERY), (2, QUERY)),
+    ((None, 500), (2, KEY_VALUE), (3, KEY_VALUE), (5, KEY_VALUE), (2, QUERY), (3, QUERY), (5, QUERY)),
+    ((None, 500), (3, KEY_VALUE), (2, KEY_VALUE), (4, KEY_VALUE), (3, QUERY), (2, QUERY), (4, QUERY)),
+    ((None, 500), (2, KEY_VALUE), (3, KEY_VALUE), (4, KEY_VALUE), (5, KEY_VALUE), (2, QUERY), (3, QUERY), (4, QUERY), (5, QUERY)),
+    ((None, 500), (3, KEY_VALUE), (2, KEY_VALUE), (5, KEY_VALUE), (4, KEY_VALUE), (3, QUERY), (2, QUERY), (5, QUERY), (4, QUERY)),
 )
 LATE_ORDER = (
     (),
@@ -69,8 +69,8 @@
     sections,
     stream_hbm, query_hbm, key_hbm, value_hbm, incoming_hbm,
     both_ref,
-    stream_own, held, gathered, result, attended,
-    load_sem, send_sem, recv_sem, query_sem, back_sem, known_sem,
+    stream_own, held, gathered, result, attended, stream_before, attended_before,
+    load_sem, send_sem, recv_sem, query_sem, back_sem, before_sem, known_sem,
 ):
     updated_ref, received_ref = both_ref.at[0], both_ref.at[1]
     key_all, value_all, query_all = (gathered.at[kind] for kind in range(3))
@@ -82,6 +82,10 @@
     width = gathered.shape[3]
     others = pl.ds(1, GROUP - 1)
     working = (me >= WORKERS[0]) & (me <= WORKERS[-1])
+    last = section == sections - 1
+    direct = (lax.rem(section, 2) == 0) & jnp.logical_not(last)
+    ahead = direct & (me == 0)
+    behind = (lax.rem(section, 2) == 1) & (me == 0)
 
     loads = [
         pltpu.make_async_copy(source, held.at[kind], load_sem.at[0])
@@ -145,6 +149,16 @@
             device_id_type=MESH,
         )
 
+    def giving_ahead(mask):
+        return pltpu.make_async_remote_copy(
+            src_ref=result.at[mask],
+            dst_ref=attended_before.at[me - WORKERS[0]],
+            send_sem=send_sem.at[1],
+            recv_sem=before_sem.at[0],
+            device_id={"section": lax.rem(section + 1, sections), "seq": base},
+            device_id_type=MESH,
+        )
+
     def passing(cols):
         return pltpu.make_async_remote_copy(
             src_ref=updated_ref.at[:, cols],
@@ -196,7 +210,22 @@
                         for kind in kinds:
                             exchange(kind, mine, theirs).start()
 
+    @pl.when(ahead)
+    def _():
+        pl.semaphore_wait(known_sem.at[0], 1)
+
     send(SEND_ORDER, [()] * len(SEND_ORDER))
+
+    @pl.when(ahead)
+    def _():
+        pltpu.make_async_remote_copy(
+            src_ref=stream_hbm,
+            dst_ref=stream_before,
+            send_sem=send_sem.at[2],
+            recv_sem=recv_sem.at[1],
+            device_id={"section": lax.rem(section + 1, sections)},
+            device_id_type=MESH,
+        ).start()
 
     factor = HEAD_SIZE ** -0.5 * LOG2_E
 
@@ -249,22 +278,42 @@
                     landed(query_all.at[pl.ds(2 * its, 2) if its else pl.ds(1, 1)], query_sem.at[its])
                 attend(pair, count)
                 for mask in range(2 * pair, 2 * (pair + count)):
-                    if mask:
+                    if mask // 2 == WORKERS[0] // 2 + number:
+
+                        @pl.when(me == mask)
+                        def _():
+                            giving_back(mask).start()
+
+                            @pl.when(direct)
+                            def _():
+                                giving_ahead(mask).start()
+
+                for mask in range(2 * pair, 2 * (pair + count)):
+                    if mask // 2 == WORKERS[0] // 2 + number:
+
+                        @pl.when(me != mask)
+                        def _():
+                            giving_back(mask).start()
+
+                    elif mask:
                         giving_back(mask).start()
 
     landed(stream_own, load_sem.at[1])
 
-    @pl.when(section < sections - 1)
+    passes = jnp.logical_not(last | ahead)
+
+    @pl.when(passes)
     def _():
         pl.semaphore_wait(known_sem.at[0], 1)
+
+    def plus(stream, piece):
+        return (stream.astype(jnp.float32) + piece.astype(jnp.float32)).astype(jnp.bfloat16)
 
     def finish(worker):
         cols = pl.ds((worker - WORKERS[0]) * width, width)
 
         def update(piece):
-            updated_ref[:, cols] = (
-                stream_own[:, cols].astype(jnp.float32) + piece.astype(jnp.float32)
-            ).astype(jnp.bfloat16)
+            updated_ref[:, cols] = plus(stream_own[:, cols], piece)
 
         @pl.when(me == worker)
         def _():
@@ -275,7 +324,7 @@
             landed(attended.at[worker - WORKERS[0]], back_sem.at[worker - WORKERS[0]])
             update(attended[worker - WORKERS[0]])
 
-        @pl.when(section < sections - 1)
+        @pl.when(passes)
         def _():
             passing(cols).start()
 
@@ -294,7 +343,14 @@
         most = pl.ds(0, (len(WORKERS) - 1) * width)
         landed(held.at[pl.ds(0, 2), :, most], send_sem.at[0])
         landed(held.at[2, :, most], send_sem.at[3])
-        landed(result.at[others], send_sem.at[1])
+
+        @pl.when(direct)
+        def _():
+            landed(result, send_sem.at[1])
+
+        @pl.when(jnp.logical_not(direct))
+        def _():
+            landed(result.at[others], send_sem.at[1])
 
     @pl.when(jnp.logical_not(working))
     def _():
@@ -304,7 +360,17 @@
     def _():
         landed(updated_ref, send_sem.at[2])
 
-    landed(received_ref, recv_sem.at[1])
+    @pl.when(behind)
+    def _():
+        landed(stream_before, recv_sem.at[1])
+        landed(attended_before, before_sem.at[0])
+        for worker in WORKERS:
+            cols = pl.ds((worker - WORKERS[0]) * width, width)
+            received_ref[:, cols] = plus(stream_before[:, cols], attended_before[worker - WORKERS[0]])
+
+    @pl.when(jnp.logical_not(behind))
+    def _():
+        landed(received_ref, recv_sem.at[1])
 
 
 def per_device(sections, stream, queries, key_rows, values, incoming):
@@ -321,11 +387,14 @@
             pltpu.VMEM((3, GROUP, rows, width), jnp.bfloat16),
             pltpu.VMEM((GROUP, rows, width), jnp.bfloat16),
             pltpu.VMEM((len(WORKERS), rows, width), jnp.bfloat16),
+            pltpu.VMEM((rows, features), jnp.bfloat16),
+            pltpu.VMEM((len(WORKERS), rows, width), jnp.bfloat16),
             pltpu.SemaphoreType.DMA((2,)),
             pltpu.SemaphoreType.DMA((4,)),
             pltpu.SemaphoreType.DMA((2,)),
             pltpu.SemaphoreType.DMA((GROUP // 2,)),
             pltpu.SemaphoreType.DMA((len(WORKERS),)),
+            pltpu.SemaphoreType.DMA((1,)),
             pltpu.SemaphoreType.REGULAR((GROUP,)),
         ],
         compiler_params=pltpu.CompilerParams(collective_id=0, has_side_effects=True),

time: 21.6 us -> 21 us (0.972)
  the two profiles are of different devices: /device:TPU:0 before, /device:TPU:3 now
where the time goes in v3:
time: 21 us; the launch traced here: 20.8 us
  Pallas kernels  19.5 us (93%)
  local copies, waits for them, and re-layouts  0.72 us (3%)
  between operations  0.64 us (3%)
    pallas_call x1, Pallas kernels, per_device(): pl.pallas_call(functools.partial(kernel, sections), out_shape=pltpu.VMEM(...  19.5 us
    slice x1, local copies, waits for them, and re-layouts, per_device(): return (both[:1], both[1:])  0.72 us

profile of v3, /device:TPU:3, one launch (start us, length us, event | category | flops | bytes accessed | tf_op | source)
XLA Modules:
  0.0 20.8 jit_solution(2406108059214276229)
XLA Ops:
  0.6 19.5 %shard_map.68 = bf16[2,64,1024]{2,1,0:T(8,128)(2,1)S(1)} custom-call(bf16[64,1024]{1,0:T(8,128)(2,1)} %bitcast.4, bf16[64,1024]{1,0:T(8,128)(2,1)} %bitcast.5, bf16[64,1024]{1,0:T(8,128)(2,1)} %bitcast.6, bf16[64,1024]{1,0:T(8,128)(2,1)} %bitcast.7, bf16[64,1024]{1,0:T(8,128)(2,1)} %incoming_hbm.1), custom_call_target="tpu_custom_call" | custom-call | tf_op jit(solution)/shard_map/pallas_call | solution.py:379
  20.1 0.7 %fusion = (bf16[1,64,1024]{2,1,0:T(8,128)(2,1)}, bf16[1,64,1024]{2,1,0:T(8,128)(2,1)}) fusion(bf16[2,64,1024]{2,1,0:T(8,128)(2,1)S(1)} %shard_map.68), kind=kLoop, calls=%fused_computation | loop fusion | bytes 524288 | tf_op jit(solution)/shard_map/slice | solution.py:402

commit v4 on v3

--- a/solution.py
+++ b/solution.py
@@ -84,8 +84,7 @@
     working = (me >= WORKERS[0]) & (me <= WORKERS[-1])
     last = section == sections - 1
     direct = (lax.rem(section, 2) == 0) & jnp.logical_not(last)
-    ahead = direct & (me == 0)
-    behind = (lax.rem(section, 2) == 1) & (me == 0)
+    behind = lax.rem(section, 2) == 1
 
     loads = [
         pltpu.make_async_copy(source, held.at[kind], load_sem.at[0])
@@ -135,17 +134,20 @@
             device_id_type=MESH,
         )
 
-    def giving_back(mask):
+    def place_at(mask):
         place = 0
         for weight in (1, 2, 4):
             bit = lax.rem(lax.div(me, weight), 2)
             place = place + weight * ((1 - bit) if mask & weight else bit)
+        return place
+
+    def giving_back(mask):
         return pltpu.make_async_remote_copy(
             src_ref=result.at[mask],
             dst_ref=attended.at[me - WORKERS[0]],
             send_sem=send_sem.at[1],
             recv_sem=back_sem.at[me - WORKERS[0]],
-            device_id={"seq": base + place},
+            device_id={"seq": base + place_at(mask)},
             device_id_type=MESH,
         )
 
@@ -153,9 +155,31 @@
         return pltpu.make_async_remote_copy(
             src_ref=result.at[mask],
             dst_ref=attended_before.at[me - WORKERS[0]],
-            send_sem=send_sem.at[1],
-            recv_sem=before_sem.at[0],
-            device_id={"section": lax.rem(section + 1, sections), "seq": base},
+            send_sem=send_sem.at[1 if mask else 4],
+            recv_sem=before_sem.at[me - WORKERS[0]],
+            device_id={"section": lax.rem(section + 1, sections), "seq": base + place_at(mask)},
+            device_id_type=MESH,
+        )
+
+    def give(mask):
+        if mask:
+
+            @pl.when(jnp.logical_not(direct) | (me == mask))
+            def _():
+                giving_back(mask).start()
+
+        @pl.when(direct)
+        def _():
+            giving_ahead(mask).start()
+
+    def handing_on(worker):
+        index = worker - WORKERS[0]
+        return pltpu.make_async_remote_copy(
+            src_ref=attended_before.at[index],
+            dst_ref=attended.at[index],
+            send_sem=send_sem.at[4],
+            recv_sem=back_sem.at[index],
+            device_id={"section": lax.rem(section + sections - 1, sections)},
             device_id_type=MESH,
         )
 
@@ -210,13 +234,13 @@
                         for kind in kinds:
                             exchange(kind, mine, theirs).start()
 
-    @pl.when(ahead)
+    @pl.when(direct)
     def _():
         pl.semaphore_wait(known_sem.at[0], 1)
 
     send(SEND_ORDER, [()] * len(SEND_ORDER))
 
-    @pl.when(ahead)
+    @pl.when(direct)
     def _():
         pltpu.make_async_remote_copy(
             src_ref=stream_hbm,
@@ -277,30 +301,22 @@
                 for its in range(pair, pair + count):
                     landed(query_all.at[pl.ds(2 * its, 2) if its else pl.ds(1, 1)], query_sem.at[its])
                 attend(pair, count)
-                for mask in range(2 * pair, 2 * (pair + count)):
-                    if mask // 2 == WORKERS[0] // 2 + number:
-
-                        @pl.when(me == mask)
-                        def _():
-                            giving_back(mask).start()
-
-                            @pl.when(direct)
-                            def _():
-                                giving_ahead(mask).start()
-
-                for mask in range(2 * pair, 2 * (pair + count)):
-                    if mask // 2 == WORKERS[0] // 2 + number:
-
-                        @pl.when(me != mask)
-                        def _():
-                            giving_back(mask).start()
-
-                    elif mask:
-                        giving_back(mask).start()
+                masks = range(2 * pair, 2 * (pair + count))
+                for mask in masks:
+
+                    @pl.when(me == mask)
+                    def _():
+                        give(mask)
+
+                for mask in masks:
+
+                    @pl.when(me != mask)
+                    def _():
+                        give(mask)
 
     landed(stream_own, load_sem.at[1])
 
-    passes = jnp.logical_not(last | ahead)
+    passes = jnp.logical_not(last | direct)
 
     @pl.when(passes)
     def _():
@@ -338,6 +354,28 @@
             for worker in order:
                 finish(worker)
 
+    @pl.when(behind)
+    def _():
+        landed(stream_before, recv_sem.at[1])
+        for worker in (2, 3, 4, 5):
+            index = worker - WORKERS[0]
+            landed(attended_before.at[index], before_sem.at[index])
+
+            @pl.when((me > 0) & (me != worker))
+            def _():
+                handing_on(worker).start()
+
+            cols = pl.ds(index * width, width)
+            received_ref[:, cols] = plus(stream_before[:, cols], attended_before[index])
+
+        @pl.when(working)
+        def _():
+            landed(attended_before.at[pl.ds(1, len(WORKERS) - 1)], send_sem.at[4])
+
+        @pl.when((me > 0) & jnp.logical_not(working))
+        def _():
+            landed(attended_before, send_sem.at[4])
+
     @pl.when(working)
     def _():
         most = pl.ds(0, (len(WORKERS) - 1) * width)
@@ -347,6 +385,7 @@
         @pl.when(direct)
         def _():
             landed(result, send_sem.at[1])
+            landed(result.at[0], send_sem.at[4])
 
         @pl.when(jnp.logical_not(direct))
         def _():
@@ -359,14 +398,6 @@
     @pl.when(section < sections - 1)
     def _():
         landed(updated_ref, send_sem.at[2])
-
-    @pl.when(behind)
-    def _():
-        landed(stream_before, recv_sem.at[1])
-        landed(attended_before, before_sem.at[0])
-        for worker in WORKERS:
-            cols = pl.ds((worker - WORKERS[0]) * width, width)
-            received_ref[:, cols] = plus(stream_before[:, cols], attended_before[worker - WORKERS[0]])
 
     @pl.when(jnp.logical_not(behind))
     def _():
@@ -390,11 +421,11 @@
             pltpu.VMEM((rows, features), jnp.bfloat16),
             pltpu.VMEM((len(WORKERS), rows, width), jnp.bfloat16),
             pltpu.SemaphoreType.DMA((2,)),
-            pltpu.SemaphoreType.DMA((4,)),
+            pltpu.SemaphoreType.DMA((5,)),
             pltpu.SemaphoreType.DMA((2,)),
             pltpu.SemaphoreType.DMA((GROUP // 2,)),
             pltpu.SemaphoreType.DMA((len(WORKERS),)),
-            pltpu.SemaphoreType.DMA((1,)),
+            pltpu.SemaphoreType.DMA((len(WORKERS),)),
             pltpu.SemaphoreType.REGULAR((GROUP,)),
         ],
         compiler_params=pltpu.CompilerParams(collective_id=0, has_side_effects=True),

time: 21 us -> 20.6 us (0.981)
  the two profiles are of different devices: /device:TPU:3 before, /device:TPU:0 now
where the time goes in v4:
time: 20.6 us; the launch traced here: 20.5 us
  Pallas kernels  19.1 us (93%)
  local copies, waits for them, and re-layouts  0.72 us (3%)
  between operations  0.64 us (3%)
    pallas_call x1, Pallas kernels, per_device(): pl.pallas_call(functools.partial(kernel, sections), out_shape=pltpu.VMEM(...  19.1 us
    slice x1, local copies, waits for them, and re-layouts, per_device(): return (both[:1], both[1:])  0.72 us

profile of v4, /device:TPU:0, one launch (start us, length us, event | category | flops | bytes accessed | tf_op | source)
XLA Modules:
  0.0 20.5 jit_solution(12371508492159770483)
XLA Ops:
  0.6 19.1 %shard_map.68 = bf16[2,64,1024]{2,1,0:T(8,128)(2,1)S(1)} custom-call(bf16[64,1024]{1,0:T(8,128)(2,1)} %bitcast.4, bf16[64,1024]{1,0:T(8,128)(2,1)} %bitcast.5, bf16[64,1024]{1,0:T(8,128)(2,1)} %bitcast.6, bf16[64,1024]{1,0:T(8,128)(2,1)} %bitcast.7, bf16[64,1024]{1,0:T(8,128)(2,1)} %incoming_hbm.1), custom_call_target="tpu_custom_call" | custom-call | tf_op jit(solution)/shard_map/pallas_call | solution.py:410
  19.7 0.7 %fusion = (bf16[1,64,1024]{2,1,0:T(8,128)(2,1)}, bf16[1,64,1024]{2,1,0:T(8,128)(2,1)}) fusion(bf16[2,64,1024]{2,1,0:T(8,128)(2,1)S(1)} %shard_map.68), kind=kLoop, calls=%fused_computation | loop fusion | bytes 524288 | tf_op jit(solution)/shard_map/slice | solution.py:433

commit v5 on v4

--- a/solution.py
+++ b/solution.py
@@ -14,8 +14,8 @@
 MESH = pl.DeviceIdType.MESH
 KEY_VALUE, QUERY, ALL = (0, 1), (2,), (0, 1, 2)
 SEND_ORDER = (
-    ((2, QUERY), (3, KEY_VALUE), (3, QUERY), (4, QUERY), (5, QUERY), (4, KEY_VALUE), (5, KEY_VALUE), (2, KEY_VALUE)),
-    ((3, QUERY), (2, KEY_VALUE), (2, QUERY), (5, QUERY), (4, QUERY), (5, KEY_VALUE), (4, KEY_VALUE), (3, KEY_VALUE)),
+    ((2, QUERY), (3, KEY_VALUE), (4, QUERY), (5, QUERY), (3, QUERY), (4, KEY_VALUE), (5, KEY_VALUE), (2, KEY_VALUE)),
+    ((3, QUERY), (2, KEY_VALUE), (5, QUERY), (4, QUERY), (2, QUERY), (5, KEY_VALUE), (4, KEY_VALUE), (3, KEY_VALUE)),
     ((4, KEY_VALUE), (5, KEY_VALUE), (3, KEY_VALUE), (4, QUERY), (5, QUERY), (3, QUERY)),
     ((5, KEY_VALUE), (4, KEY_VALUE), (2, KEY_VALUE), (5, QUERY), (4, QUERY), (2, QUERY)),
     ((2, KEY_VALUE), (3, KEY_VALUE), (5, KEY_VALUE), (2, QUERY), (3, QUERY), (5, QUERY)),
@@ -49,7 +49,7 @@
     (),
     (),
 )
-SERVE_ORDER = (((1, 1), (3, 1), (2, 1), (0, 1)), ((2, 1), (3, 1), (0, 1), (1, 1)))
+SERVE_ORDER = (((1, 1), (3, 1), (2, 1), (0, 1)), ((2, 1), (0, 1), (3, 1), (1, 1)))
 FINISH_ORDER = ((2, 3, 4, 5), (2, 3, 4, 5), (2, 3, 4, 5), (2, 3, 4, 5))
 
 

time: 20.6 us -> 20.6 us (level)
  no operation moved by 1% of the time
where the time goes in v5:
time: 20.6 us; the launch traced here: 20.4 us
  Pallas kernels  19.1 us (93%)
  local copies, waits for them, and re-layouts  0.72 us (3%)
  between operations  0.64 us (3%)
    pallas_call x1, Pallas kernels, per_device(): pl.pallas_call(functools.partial(kernel, sections), out_shape=pltpu.VMEM(...  19.1 us
    slice x1, local copies, waits for them, and re-layouts, per_device(): return (both[:1], both[1:])  0.72 us

profile of v5, /device:TPU:0, one launch (start us, length us, event | category | flops | bytes accessed | tf_op | source)
XLA Modules:
  0.0 20.4 jit_solution(8906955158940102134)
XLA Ops:
  0.6 19.1 %shard_map.68 = bf16[2,64,1024]{2,1,0:T(8,128)(2,1)S(1)} custom-call(bf16[64,1024]{1,0:T(8,128)(2,1)} %bitcast.4, bf16[64,1024]{1,0:T(8,128)(2,1)} %bitcast.5, bf16[64,1024]{1,0:T(8,128)(2,1)} %bitcast.6, bf16[64,1024]{1,0:T(8,128)(2,1)} %bitcast.7, bf16[64,1024]{1,0:T(8,128)(2,1)} %incoming_hbm.1), custom_call_target="tpu_custom_call" | custom-call | tf_op jit(solution)/shard_map/pallas_call | solution.py:410
  19.7 0.7 %fusion = (bf16[1,64,1024]{2,1,0:T(8,128)(2,1)}, bf16[1,64,1024]{2,1,0:T(8,128)(2,1)}) fusion(bf16[2,64,1024]{2,1,0:T(8,128)(2,1)S(1)} %shard_map.68), kind=kLoop, calls=%fused_computation | loop fusion | bytes 524288 | tf_op jit(solution)/shard_map/slice | solution.py:433

commit v6 on v5

--- a/solution.py
+++ b/solution.py
@@ -16,16 +16,16 @@
 SEND_ORDER = (
     ((2, QUERY), (3, KEY_VALUE), (4, QUERY), (5, QUERY), (3, QUERY), (4, KEY_VALUE), (5, KEY_VALUE), (2, KEY_VALUE)),
     ((3, QUERY), (2, KEY_VALUE), (5, QUERY), (4, QUERY), (2, QUERY), (5, KEY_VALUE), (4, KEY_VALUE), (3, KEY_VALUE)),
-    ((4, KEY_VALUE), (5, KEY_VALUE), (3, KEY_VALUE), (4, QUERY), (5, QUERY), (3, QUERY)),
-    ((5, KEY_VALUE), (4, KEY_VALUE), (2, KEY_VALUE), (5, QUERY), (4, QUERY), (2, QUERY)),
+    ((4, KEY_VALUE), (5, KEY_VALUE), (3, KEY_VALUE), (3, QUERY), (4, QUERY), (5, QUERY)),
+    ((5, KEY_VALUE), (4, KEY_VALUE), (2, KEY_VALUE), (2, QUERY), (5, QUERY), (4, QUERY)),
     ((2, KEY_VALUE), (3, KEY_VALUE), (5, KEY_VALUE), (2, QUERY), (3, QUERY), (5, QUERY)),
     ((3, KEY_VALUE), (2, KEY_VALUE), (4, KEY_VALUE), (3, QUERY), (2, QUERY), (4, QUERY)),
     ((2, KEY_VALUE), (3, KEY_VALUE), (4, KEY_VALUE), (5, KEY_VALUE), (2, QUERY), (3, QUERY), (4, QUERY), (5, QUERY)),
     ((3, KEY_VALUE), (2, KEY_VALUE), (5, KEY_VALUE), (4, KEY_VALUE), (3, QUERY), (2, QUERY), (5, QUERY), (4, QUERY)),
     ((None, 500), (2, KEY_VALUE), (3, KEY_VALUE), (4, KEY_VALUE), (5, KEY_VALUE), (4, QUERY), (5, QUERY), (2, QUERY), (3, QUERY)),
     ((None, 500), (3, KEY_VALUE), (2, KEY_VALUE), (5, KEY_VALUE), (4, KEY_VALUE), (5, QUERY), (4, QUERY), (3, QUERY), (2, QUERY)),
-    ((None, 500), (4, KEY_VALUE), (5, KEY_VALUE), (3, KEY_VALUE), (4, QUERY), (5, QUERY), (3, QUERY)),
-    ((None, 500), (5, KEY_VALUE), (4, KEY_VALUE), (2, KEY_VALUE), (5, QUERY), (4, QUERY), (2, QUERY)),
+    ((None, 500), (4, KEY_VALUE), (5, KEY_VALUE), (3, KEY_VALUE), (3, QUERY), (4, QUERY), (5, QUERY)),
+    ((None, 500), (5, KEY_VALUE), (4, KEY_VALUE), (2, KEY_VALUE), (2, QUERY), (5, QUERY), (4, QUERY)),
     ((None, 500), (2, KEY_VALUE), (3, KEY_VALUE), (5, KEY_VALUE), (2, QUERY), (3, QUERY), (5, QUERY)),
     ((None, 500), (3, KEY_VALUE), (2, KEY_VALUE), (4, KEY_VALUE), (3, QUERY), (2, QUERY), (4, QUERY)),
     ((None, 500), (2, KEY_VALUE), (3, KEY_VALUE), (4, KEY_VALUE), (5, KEY_VALUE), (2, QUERY), (3, QUERY), (4, QUERY), (5, QUERY)),

time: 20.6 us -> 20.6 us (level)
  no operation moved by 1% of the time
where the time goes in v6:
time: 20.6 us; the launch traced here: 20.4 us
  Pallas kernels  19.1 us (93%)
  local copies, waits for them, and re-layouts  0.72 us (3%)
  between operations  0.64 us (3%)
    pallas_call x1, Pallas kernels, per_device(): pl.pallas_call(functools.partial(kernel, sections), out_shape=pltpu.VMEM(...  19.1 us
    slice x1, local copies, waits for them, and re-layouts, per_device(): return (both[:1], both[1:])  0.72 us

profile of v6, /device:TPU:0, one launch (start us, length us, event | category | flops | bytes accessed | tf_op | source)
XLA Modules:
  0.0 20.4 jit_solution(5688886438635926364)
XLA Ops:
  0.6 19.1 %shard_map.68 = bf16[2,64,1024]{2,1,0:T(8,128)(2,1)S(1)} custom-call(bf16[64,1024]{1,0:T(8,128)(2,1)} %bitcast.4, bf16[64,1024]{1,0:T(8,128)(2,1)} %bitcast.5, bf16[64,1024]{1,0:T(8,128)(2,1)} %bitcast.6, bf16[64,1024]{1,0:T(8,128)(2,1)} %bitcast.7, bf16[64,1024]{1,0:T(8,128)(2,1)} %incoming_hbm.1), custom_call_target="tpu_custom_call" | custom-call | tf_op jit(solution)/shard_map/pallas_call | solution.py:410
  19.7 0.7 %fusion = (bf16[1,64,1024]{2,1,0:T(8,128)(2,1)}, bf16[1,64,1024]{2,1,0:T(8,128)(2,1)}) fusion(bf16[2,64,1024]{2,1,0:T(8,128)(2,1)S(1)} %shard_map.68), kind=kLoop, calls=%fused_computation | loop fusion | bytes 524288 | tf_op jit(solution)/shard_map/slice | solution.py:433
